TPU v7x, 128 devices: a whole 4x4x4 slice. The times are simulated.
128 devices in a mesh: head: 16 (over z, y), batch: 8 (over x, core).
Axes of the slice: x: 4, y: 4, z: 4, core: 2. Of those that a mesh axis runs over, the one named last changes fastest.
Arguments:
- incoming_hidden_stream: bfloat16 [1024, 4096], P('batch'), may hold values from -6 to 6
- reception_projection: bfloat16 [4096, 4096], P(None, 'head'), may hold values from -0.09375 to 0.09375
- address_projection: bfloat16 [4096, 4096], P(None, 'head'), may hold values from -0.09375 to 0.09375
- payload_projection: bfloat16 [4096, 4096], P(None, 'head'), may hold values from -0.09375 to 0.09375
- sigmoid_filter_matrix: bfloat16 [4096, 4096], P(None, 'head'), may hold values from -0.09375 to 0.09375
- forgetting_speed: float32 [1024, 4096], P('batch', 'head'), may hold values from 0.01 to 1.5
- adaptation_step_size: float32 [1024, 4096], P('batch', 'head'), may hold values from 0 to 1
- diagonal_boost: float32 [4096], P('head'), may hold values from -0.6 to 0.6
- subspace_standardize_scale: float32 [4096], P('head'), may hold values from 0.5 to 2
- recurrent_memory_matrix: float32 [128, 64, 64, 64], P('batch', 'head'), may hold values from -6 to 6
- emission_projection: bfloat16 [4096, 4096], P('head'), may hold values from -0.09375 to 0.09375
- closing_standardize_scale: float32 [4096], replicated, may hold values from 0.7 to 2
- lexicon_projection: bfloat16 [4096, 65536], P(None, ('head', 'batch')), may hold values from -32 to 32
- proposed_tokens_list: int32 [128, 8], P('batch'), may hold values from 0 to 65535
- threshold_milli_nats: int32 [128, 8], P('batch'), may hold values from -22000 to -10001
Outputs:
- new_state: float32 [128, 64, 64, 64], P('batch', 'head')
- margin: float32 [128, 8], P('batch')
- accept: float32 [128, 8], P('batch')
All inputs are finite; a program needn't handle non-finite values.
Results may differ from a plain program's by a relative error of at most 0.0017.
Values may be sent and summed in bfloat16 or wider, within the bound.
A program may use at most 128 MiB of HBM per device.

v0:
```python
import math
import jax
import jax.numpy as jnp
from jax import lax
from jax.sharding import Mesh
from jax.sharding import PartitionSpec as P

HEAD = ("head_0", "head_1")
HEAD_BATCH = ("head_0", "head_1", "batch")


def in_blocks(x, dim, size):
    before, after = (x.shape[:dim], x.shape[dim + 1 :])
    return jnp.moveaxis(x.reshape(*before, size, -1, *after), dim, 0)


def sent_and_summed(x, axis, dim):
    size = lax.axis_size(axis)
    parts = lax.all_to_all(in_blocks(x, dim, size), axis, 0, 0, tiled=True)
    return jnp.sum(parts, axis=0)


def by_axis(x, axes):
    for axis in axes:
        x = lax.psum(x, axis)
    return x


def joined_along(parts, dim):
    parts = jnp.moveaxis(parts, 0, dim)
    shape = parts.shape
    return parts.reshape(*shape[:dim], shape[dim] * shape[dim + 1], *shape[dim + 2 :])


def sent_to_all(x, axis):
    copies = jnp.broadcast_to(x, (lax.axis_size(axis), *x.shape))
    return lax.all_to_all(copies, axis, split_axis=0, concat_axis=0, tiled=True)


def gathered_copies(x, axis, dim):
    return joined_along(sent_to_all(x, axis), dim)


def gathered_once(x, axis):
    leaves = jax.tree.leaves(x)
    sequence = sorted(range(len(leaves)), key=lambda k: -leaves[k].size)
    width = (1, *leaves[sequence[0]].shape)[-1]
    lines = [
        jnp.pad(leaves[k].reshape(-1), (0, -leaves[k].size % width)).reshape(-1, width)
        for k in sequence
    ]
    both, at, found = (sent_to_all(jnp.concatenate(lines), axis), 0, {})
    for k, line in zip(sequence, lines):
        share = both[:, at : at + len(line)].reshape(len(both), -1)
        found[k] = share[:, : leaves[k].size].reshape(-1, *leaves[k].shape)
        at += len(line)
    numbers = iter(range(len(leaves)))
    return jax.tree.map(lambda _: found[next(numbers)], x)


def combined_pairwise(pieces, combine):
    while len(jax.tree.leaves(pieces)[0]) > 1:
        pieces = jax.vmap(combine)(
            *(jax.tree.map(lambda part: part[side::2], pieces) for side in (0, 1))
        )
    return jax.tree.map(lambda part: part[0], pieces)


def combined_all(x, axis, combine):
    pieces = gathered_once(x, axis)
    return combined_pairwise(pieces, combine)


def gathered_by_type(x, axis):
    leaves, found = (jax.tree.leaves(x), {})
    for initial, a in enumerate(leaves):
        if initial not in found:
            alike = [k for k, b in enumerate(leaves) if b.dtype == a.dtype]
            got = (
                gathered_once([leaves[k] for k in alike], axis)
                if len(alike) > 1
                else [sent_to_all(a, axis)]
            )
            for k, b in zip(alike, got):
                found[k] = b
    numbers = iter(range(len(leaves)))
    return jax.tree.map(lambda _: found[next(numbers)], x)


def merged(x, axis, combine):
    pieces = gathered_by_type(x, axis)
    return combined_pairwise(pieces, combine)


def advance(start, reception_vectors, address_vectors, payload_vectors, decay, rate):
    unit = (
        address_vectors
        * lax.rsqrt(jnp.mean(address_vectors * address_vectors, -1, keepdims=True) + 1e-06)
        / math.sqrt(address_vectors.shape[-1])
    )
    inputs = tuple(
        (
            jnp.moveaxis(item, 1, 0)
            for item in (reception_vectors, address_vectors, payload_vectors, decay, unit, rate)
        )
    )

    def step(current, pieces):
        recept_now, keys_now, values_now, decay_now, unit_now, rate_now = pieces
        recall = jnp.einsum("bhij,bhj->bhi", current, unit_now, precision=lax.Precision.HIGHEST)
        current = (
            current * decay_now[:, :, None, :]
            - recall[:, :, :, None] * (unit_now * rate_now)[:, :, None, :]
            + values_now[:, :, :, None] * keys_now[:, :, None, :]
        )
        output = jnp.einsum("bhij,bhj->bhi", current, recept_now, precision=lax.Precision.HIGHEST)
        return (current, output)

    final, outputs = lax.scan(step, start, inputs)
    return (final, jnp.moveaxis(outputs, 0, 1))


def combine_stats(first, second):
    top = jnp.maximum(first[0], second[0])
    summed = first[1] * jnp.exp(first[0] - top) + second[1] * jnp.exp(second[0] - top)
    return (top, summed, first[2] + second[2])


def local_stats(logits, ids_flat, offset):
    peak = jnp.max(logits, -1)
    total = jnp.sum(jnp.exp(logits - peak[:, None]), -1)
    column = lax.broadcasted_iota(jnp.int32, logits.shape, 1)
    target = jnp.sum(jnp.where(column == (ids_flat - offset)[:, None], logits, 0.0), -1)
    return (peak, total, target)


def shards(
    incoming_hidden_stream,
    reception_projection,
    address_projection,
    payload_projection,
    sigmoid_filter_matrix,
    forgetting_speed,
    adaptation_step_size,
    diagonal_boost,
    subspace_standardize_scale,
    recurrent_memory_matrix,
    emission_projection,
    closing_standardize_scale,
    lexicon_projection,
    proposed_tokens_list,
    threshold_milli_nats,
):
    seq_dev, draft_len = proposed_tokens_list.shape
    lanes_on_shard, subspace_size = (
        recurrent_memory_matrix.shape[1],
        recurrent_memory_matrix.shape[2],
    )
    tok_dev = seq_dev * draft_len
    width = incoming_hidden_stream.shape[1]
    shape4 = (seq_dev, draft_len, lanes_on_shard, subspace_size)
    reception_vectors = jnp.dot(
        incoming_hidden_stream, reception_projection, preferred_element_type=jnp.float32
    ).reshape(shape4)
    address_vectors = jnp.dot(
        incoming_hidden_stream, address_projection, preferred_element_type=jnp.float32
    ).reshape(shape4)
    payload_vectors = jnp.dot(
        incoming_hidden_stream, payload_projection, preferred_element_type=jnp.float32
    ).reshape(shape4)
    gate = jnp.dot(
        incoming_hidden_stream, sigmoid_filter_matrix, preferred_element_type=jnp.float32
    )
    decay = jnp.exp(-forgetting_speed).reshape(shape4)
    rate = adaptation_step_size.reshape(shape4)
    new_state, wkv = advance(
        recurrent_memory_matrix, reception_vectors, address_vectors, payload_vectors, decay, rate
    )
    center = wkv - jnp.mean(wkv, -1, keepdims=True)
    interpolated_embedding = (
        center
        * lax.rsqrt(jnp.mean(center * center, -1, keepdims=True) + 1e-05)
        * subspace_standardize_scale.reshape(lanes_on_shard, subspace_size)
    )
    interpolated_embedding = (
        interpolated_embedding
        + jnp.sum(
            reception_vectors
            * address_vectors
            * diagonal_boost.reshape(lanes_on_shard, subspace_size),
            -1,
            keepdims=True,
        )
        * payload_vectors
    )
    gated = (
        interpolated_embedding.reshape(tok_dev, lanes_on_shard * subspace_size)
        * jax.nn.sigmoid(gate)
    ).astype(jnp.bfloat16)
    partial_out = jnp.dot(gated, emission_projection, preferred_element_type=jnp.float32)
    share = sent_and_summed(partial_out, HEAD, 1)
    cols = share.shape[1]
    begin = lax.axis_index(HEAD) * cols
    residual = (
        lax.dynamic_slice_in_dim(incoming_hidden_stream, begin, cols, 1).astype(jnp.float32) + share
    )
    moment_one, moment_two = (
        by_axis(jnp.sum(residual, -1), HEAD),
        by_axis(jnp.sum(residual * residual, -1), HEAD),
    )
    mean_row = moment_one / width
    variance = moment_two / width - mean_row * mean_row
    gain_part = lax.dynamic_slice_in_dim(closing_standardize_scale, begin, cols, 0)
    normed_part = (
        (residual - mean_row[:, None]) * lax.rsqrt(variance + 1e-05)[:, None] * gain_part
    ).astype(jnp.bfloat16)
    normed = gathered_copies(normed_part, HEAD, 1)
    every, every_ids = (
        lax.all_gather(normed, "batch", axis=0, tiled=True),
        lax.all_gather(proposed_tokens_list, "batch", axis=0, tiled=True),
    )
    logits = jnp.dot(every, lexicon_projection, preferred_element_type=jnp.float32)
    vcols = lexicon_projection.shape[1]
    offset = (lax.axis_index(HEAD) * lax.axis_size("batch") + lax.axis_index("batch")) * vcols
    peak, total, target = local_stats(logits, every_ids.reshape(-1), offset)
    peak, total, target = combined_all((peak, total, target), "batch", combine_stats)
    row_begin = lax.axis_index("batch") * tok_dev
    peak = lax.dynamic_slice_in_dim(peak, row_begin, tok_dev, 0)
    total = lax.dynamic_slice_in_dim(total, row_begin, tok_dev, 0)
    target = lax.dynamic_slice_in_dim(target, row_begin, tok_dev, 0)
    top, summed, target = merged((peak, total, target), HEAD, combine_stats)
    logprob = target - (top + jnp.log(summed))
    margin = logprob.reshape(seq_dev, draft_len) - threshold_milli_nats.astype(jnp.float32) / 1000.0
    accept = jnp.cumprod(jax.nn.sigmoid(margin * 0.5), axis=1)
    return (new_state, margin, accept)


def solution(mesh):
    split = Mesh(mesh.devices.reshape(4, 4, mesh.shape["batch"]), ("head_0", "head_1", "batch"))
    return jax.shard_map(
        shards,
        mesh=split,
        in_specs=(
            P("batch", None),
            P(None, HEAD),
            P(None, HEAD),
            P(None, HEAD),
            P(None, HEAD),
            P("batch", HEAD),
            P("batch", HEAD),
            P(HEAD),
            P(HEAD),
            P("batch", HEAD, None, None),
            P(HEAD, None),
            P(),
            P(None, HEAD_BATCH),
            P("batch", None),
            P("batch", None),
        ),
        out_specs=(P("batch", HEAD, None, None), P("batch", None), P("batch", None)),
        check_vma=False,
    )
```

profile of v0, /device:TPU:0, one launch (start us, length us, event | category | flops | bytes accessed | tf_op | source)
XLA Modules:
  0.0 318.9 jit_solution(11417522193714851282)
XLA Ops:
  29.0 105.4 %while.12 = (s32[]{:T(128)}, f32[16,4,64,64]{3,2,1,0:T(8,128)}, f32[8,16,4,64]{3,2,1,0:T(4,128)S(1)}, f32[8,16,4,64]{3,2,0,1:T(4,128)}, f32[8,16,4,64]{3,2,1,0:T...) while((s32[]{:T(128)}, f32[16,4,64,64]{3,2,1,0:T(8,128)}, ...), condition=%wide.region_2.3_spmd, body=%wide.region_1.2_spmd.sunk | while | flops 7606274 | bytes 13009081 | solution.py:119
  31.5 4.9 %fusion.54 = f32[16,4,1,64]{3,2,1,0:T(1,128)S(1)} fusion(f32[16,4,64,1]{2,3,1,0:T(1,128)S(1)} %bitcast.118, f32[16,4,64,64]{3,2,1,0:T(8,128)} %get-tuple-element.245), kind=kOutput, calls=%fused_computation.79.clone.1 | convolution fusion | flops 3145728 | bytes 1081344 | tf_op jit(solution)/shard_map/while/body/eval_jaxpr/bhij,bhj->bhi/dot_general | solution.py:110
  44.7 4.9 %fusion.54 = f32[16,4,1,64]{3,2,1,0:T(1,128)S(1)} fusion(f32[16,4,64,1]{2,3,1,0:T(1,128)S(1)} %bitcast.118, f32[16,4,64,64]{3,2,1,0:T(8,128)} %get-tuple-element.245), kind=kOutput, calls=%fused_computation.79.clone.1 | convolution fusion | flops 3145728 | bytes 1081344 | tf_op jit(solution)/shard_map/while/body/eval_jaxpr/bhij,bhj->bhi/dot_general | solution.py:110
  52.0 3.3 %fusion.55 = f32[16,4,1,64]{3,2,1,0:T(1,128)S(1)} fusion(f32[16,4,64,64]{3,2,1,0:T(8,128)S(1)} %multiply_add_fusion.8, f32[16,4,64,1]{2,3,1,0:T(1,128)S(1)} %bitcast.117), kind=kOutput, calls=%fused_computation.80.clone.1 | convolution fusion | flops 3145728 | bytes 1081344 | tf_op jit(solution)/shard_map/while/body/eval_jaxpr/bhij,bhj->bhi/dot_general | solution.py:116
  57.9 4.9 %fusion.54 = f32[16,4,1,64]{3,2,1,0:T(1,128)S(1)} fusion(f32[16,4,64,1]{2,3,1,0:T(1,128)S(1)} %bitcast.118, f32[16,4,64,64]{3,2,1,0:T(8,128)} %get-tuple-element.245), kind=kOutput, calls=%fused_computation.79.clone.1 | convolution fusion | flops 3145728 | bytes 1081344 | tf_op jit(solution)/shard_map/while/body/eval_jaxpr/bhij,bhj->bhi/dot_general | solution.py:110
  71.0 4.9 %fusion.54 = f32[16,4,1,64]{3,2,1,0:T(1,128)S(1)} fusion(f32[16,4,64,1]{2,3,1,0:T(1,128)S(1)} %bitcast.118, f32[16,4,64,64]{3,2,1,0:T(8,128)} %get-tuple-element.245), kind=kOutput, calls=%fused_computation.79.clone.1 | convolution fusion | flops 3145728 | bytes 1081344 | tf_op jit(solution)/shard_map/while/body/eval_jaxpr/bhij,bhj->bhi/dot_general | solution.py:110
  78.3 3.3 %fusion.55 = f32[16,4,1,64]{3,2,1,0:T(1,128)S(1)} fusion(f32[16,4,64,64]{3,2,1,0:T(8,128)S(1)} %multiply_add_fusion.8, f32[16,4,64,1]{2,3,1,0:T(1,128)S(1)} %bitcast.117), kind=kOutput, calls=%fused_computation.80.clone.1 | convolution fusion | flops 3145728 | bytes 1081344 | tf_op jit(solution)/shard_map/while/body/eval_jaxpr/bhij,bhj->bhi/dot_general | solution.py:116
  84.2 4.9 %fusion.54 = f32[16,4,1,64]{3,2,1,0:T(1,128)S(1)} fusion(f32[16,4,64,1]{2,3,1,0:T(1,128)S(1)} %bitcast.118, f32[16,4,64,64]{3,2,1,0:T(8,128)} %get-tuple-element.245), kind=kOutput, calls=%fused_computation.79.clone.1 | convolution fusion | flops 3145728 | bytes 1081344 | tf_op jit(solution)/shard_map/while/body/eval_jaxpr/bhij,bhj->bhi/dot_general | solution.py:110
  97.4 4.9 %fusion.54 = f32[16,4,1,64]{3,2,1,0:T(1,128)S(1)} fusion(f32[16,4,64,1]{2,3,1,0:T(1,128)S(1)} %bitcast.118, f32[16,4,64,64]{3,2,1,0:T(8,128)} %get-tuple-element.245), kind=kOutput, calls=%fused_computation.79.clone.1 | convolution fusion | flops 3145728 | bytes 1081344 | tf_op jit(solution)/shard_map/while/body/eval_jaxpr/bhij,bhj->bhi/dot_general | solution.py:110
  110.6 4.9 %fusion.54 = f32[16,4,1,64]{3,2,1,0:T(1,128)S(1)} fusion(f32[16,4,64,1]{2,3,1,0:T(1,128)S(1)} %bitcast.118, f32[16,4,64,64]{3,2,1,0:T(8,128)} %get-tuple-element.245), kind=kOutput, calls=%fused_computation.79.clone.1 | convolution fusion | flops 3145728 | bytes 1081344 | tf_op jit(solution)/shard_map/while/body/eval_jaxpr/bhij,bhj->bhi/dot_general | solution.py:110
  123.8 4.9 %fusion.54 = f32[16,4,1,64]{3,2,1,0:T(1,128)S(1)} fusion(f32[16,4,64,1]{2,3,1,0:T(1,128)S(1)} %bitcast.118, f32[16,4,64,64]{3,2,1,0:T(8,128)} %get-tuple-element.245), kind=kOutput, calls=%fused_computation.79.clone.1 | convolution fusion | flops 3145728 | bytes 1081344 | tf_op jit(solution)/shard_map/while/body/eval_jaxpr/bhij,bhj->bhi/dot_general | solution.py:110
  139.9 4.2 %fusion.5 = f32[128,4096]{1,0:T(8,128)} fusion(bf16[256,4096]{1,0:T(8,128)(2,1)S(1)} %copy-done, f32[128,256]{1,0:T(8,128)S(1)} %reshape.129, bf16[128,4096]{1,0:T(8,128)(2,1)S(1)} %copy-done.3, bf16[4096,256]{1,0:T(8,128)(2,1)} %param.21), kind=kOutput, calls=%fused_computation.18 | convolution fusion | flops 537034752 | bytes 7471104 | tf_op jit(solution)/shard_map/dot_general | solution.py:200
  147.3 8.2 %all-to-all-start = ((f32[16,128,256]{2,1,0:T(8,128)}), f32[16,128,256]{2,1,0:T(8,128)}, u32[]{:S(2)}, u32[]{:S(2)}) async-start(f32[16,128,256]{2,1,0:T(8,128)} %bitcast.113), calls=%async_computation | async-start | bytes 4194304 | tf_op jit(solution)/shard_map/all_to_all | solution.py:19
  156.4 31.0 %all-to-all-done = f32[16,128,256]{2,1,0:T(8,128)} async-done(((f32[16,128,256]{2,1,0:T(8,128)}), f32[16,128,256]{2,1,0:T(8,128)}, u32[]{:S(2)}, u32[]{:S(2)}) %all-to-all-start) | async-done | bytes 2097184 | tf_op jit(solution)/shard_map/all_to_all | solution.py:19
  189.2 9.5 %all-reduce.1 = (f32[128]{0:T(128)S(1)}, f32[128]{0:T(128)S(1)}) all-reduce(f32[128]{0:T(128)S(1)} %get-tuple-element.107, f32[128]{0:T(128)S(1)} %get-tuple-element.106), channel_id=1, replica_groups=mesh['head_0'=4,'head_1'=4,'batch'=8] {'head_0'}, use_global_device_ids=true, to_apply=%region_11.12 | all-reduce | flops 256 | bytes 2048 | tf_op jit(solution)/shard_map/psum | solution.py:25
  198.7 7.7 %all-reduce = (f32[128]{0:T(128)S(1)}, f32[128]{0:T(128)S(1)}) all-reduce(f32[128]{0:T(128)S(1)} %get-tuple-element.130, f32[128]{0:T(128)S(1)} %get-tuple-element.131), channel_id=1, replica_groups=mesh['head_0'=4,'head_1'=4,'batch'=8] {'head_1'}, use_global_device_ids=true, to_apply=%region_12.13 | all-reduce | flops 256 | bytes 2048 | tf_op jit(solution)/shard_map/psum | solution.py:25
  206.9 16.6 %all_to_all.20 = bf16[16,128,256]{1,2,0:T(8,128)(2,1)} all-to-all(bf16[16,128,256]{1,2,0:T(8,128)(2,1)S(1)} %broadcast_in_dim.21), channel_id=1, replica_groups=mesh['head_0'=4,'head_1'=4,'batch'=8] {'head_0','head_1'}, dimensions={0} | all-to-all | bytes 2097152 | tf_op jit(solution)/shard_map/all_to_all | solution.py:37
  223.5 13.3 %all-gather = s32[8,16,8]{1,2,0:T(8,128)S(1)} all-gather(s32[1,16,8]{1,2,0:T(8,128)S(1)} %bitcast.136), channel_id=1, replica_groups=mesh['head_0'=4,'head_1'=4,'batch'=8] {'batch'}, dimensions={0}, use_global_device_ids=true | all-gather | bytes 4608 | tf_op jit(solution)/shard_map/all_gather | solution.py:220
  237.0 37.6 %all-gather.3.cloned.1.call-done = bf16[1024,4096]{0,1:T(8,128)(2,1)} async-done(((bf16[128,4096]{0,1:T(8,128)(2,1)}), bf16[1024,4096]{0,1:T(8,128)(2,1)}) %all-gather.3.cloned.1.call-update) | async-done | bytes 8388624 | tf_op jit(solution)/shard_map/all_gather | solution.py:219
  274.6 8.3 %fusion.23 = (f32[1024]{0:T(1024)S(1)}, f32[1024,512]{0,1:T(8,128)S(1)}) fusion(bf16[1024,4096]{0,1:T(8,128)(2,1)} %all-gather.3.cloned.1.call-done, bf16[4096,512]{1,0:T(8,128)(2,1)} %param.29), kind=kOutput, calls=%fused_computation.78 | convolution fusion | flops 4295490560 | bytes 14684160 | tf_op jit(solution)/shard_map/dot_general | solution.py:222
  284.1 4.0 %all-to-all-start.2 = ((f32[8,3,1024]{2,1,0:T(4,128)}), f32[8,3,1024]{2,1,0:T(4,128)S(1)}, u32[]{:S(2)}, u32[]{:S(2)}) async-start(f32[8,3,1024]{2,1,0:T(4,128)} %broadcast_in_dim.23), calls=%async_computation.2 | async-start | bytes 262144 | tf_op jit(solution)/shard_map/all_to_all | solution.py:37
  288.1 6.1 %all-to-all-done.2 = f32[8,3,1024]{2,1,0:T(4,128)S(1)} async-done(((f32[8,3,1024]{2,1,0:T(4,128)}), f32[8,3,1024]{2,1,0:T(4,128)S(1)}, u32[]{:S(2)}, u32[]{:S(2)}) %all-to-all-start.2) | async-done | bytes 98336 | tf_op jit(solution)/shard_map/all_to_all | solution.py:37
  295.4 6.9 %all-to-all-start.3 = ((f32[16,3,128]{2,1,0:T(4,128)}), f32[16,3,128]{2,1,0:T(4,128)S(1)}, u32[]{:S(2)}, u32[]{:S(2)}) async-start(f32[16,3,128]{2,1,0:T(4,128)} %broadcast_in_dim.25), calls=%async_computation.3 | async-start | bytes 65536 | tf_op jit(solution)/shard_map/all_to_all | solution.py:37
  302.5 7.5 %all-to-all-done.3 = f32[16,3,128]{2,1,0:T(4,128)S(1)} async-done(((f32[16,3,128]{2,1,0:T(4,128)}), f32[16,3,128]{2,1,0:T(4,128)S(1)}, u32[]{:S(2)}, u32[]{:S(2)}) %all-to-all-start.3) | async-done | bytes 24608 | tf_op jit(solution)/shard_map/all_to_all | solution.py:37
  (206 shorter events, 97.0 us)
Async XLA Ops:
  7.2 132.8 %copy-start = (bf16[256,4096]{1,0:T(8,128)(2,1)S(1)}, bf16[256,4096]{1,0:T(8,128)(2,1)}, u32[]{:S(2)}) copy-start(bf16[256,4096]{1,0:T(8,128)(2,1)} %param.27) | copy-start | bytes 6291460
  7.2 5.1 %copy-start.3 = (bf16[128,4096]{1,0:T(8,128)(2,1)S(1)}, bf16[128,4096]{1,0:T(8,128)(2,1)}, u32[]{:S(2)}) copy-start(bf16[128,4096]{1,0:T(8,128)(2,1)} %param.17) | copy-start | bytes 3145732
  14.3 3.7 %copy-start.7 = (f32[256]{0:T(256)S(1)}, f32[256]{0:T(256)}, u32[]{:S(2)}) copy-start(f32[256]{0:T(256)} %param.24) | copy-start | bytes 3076
  29.0 105.5 %copy-start.4 = (f32[16,8,4]{2,1,0:T(8,128)S(1)}, f32[16,8,4]{2,1,0:T(8,128)}, u32[]{:S(2)}) copy-start(f32[16,8,4]{2,1,0:T(8,128)} %get-tuple-element.108) | copy-start | bytes 6148
  29.0 106.1 %copy-start.8 = (f32[256]{0:T(256)S(1)}, f32[256]{0:T(256)}, u32[]{:S(2)}) copy-start(f32[256]{0:T(256)} %param.25) | copy-start | bytes 3076
  29.0 8.2 %copy-start.1 = (f32[16,4,64,64]{3,2,1,0:T(8,128)S(1)}, f32[16,4,64,64]{3,2,1,0:T(8,128)}, u32[]{:S(2)}) copy-start(f32[16,4,64,64]{3,2,1,0:T(8,128)} %get-tuple-element.245) | copy-start | bytes 3145732 | tf_op jit(solution)/shard_map/while
  38.8 3.4 %copy-start.2 = (f32[16,4,64,64]{3,2,1,0:T(8,128)}, f32[16,4,64,64]{3,2,1,0:T(8,128)S(1)}, u32[]{:S(2)}) copy-start(f32[16,4,64,64]{3,2,1,0:T(8,128)S(1)} %multiply_add_fusion.8) | copy-start | bytes 3145732 | tf_op jit(solution)/shard_map/while
  42.2 8.2 %copy-start.1 = (f32[16,4,64,64]{3,2,1,0:T(8,128)S(1)}, f32[16,4,64,64]{3,2,1,0:T(8,128)}, u32[]{:S(2)}) copy-start(f32[16,4,64,64]{3,2,1,0:T(8,128)} %get-tuple-element.245) | copy-start | bytes 3145732 | tf_op jit(solution)/shard_map/while
  51.9 3.4 %copy-start.2 = (f32[16,4,64,64]{3,2,1,0:T(8,128)}, f32[16,4,64,64]{3,2,1,0:T(8,128)S(1)}, u32[]{:S(2)}) copy-start(f32[16,4,64,64]{3,2,1,0:T(8,128)S(1)} %multiply_add_fusion.8) | copy-start | bytes 3145732 | tf_op jit(solution)/shard_map/while
  55.3 8.2 %copy-start.1 = (f32[16,4,64,64]{3,2,1,0:T(8,128)S(1)}, f32[16,4,64,64]{3,2,1,0:T(8,128)}, u32[]{:S(2)}) copy-start(f32[16,4,64,64]{3,2,1,0:T(8,128)} %get-tuple-element.245) | copy-start | bytes 3145732 | tf_op jit(solution)/shard_map/while
  68.5 8.2 %copy-start.1 = (f32[16,4,64,64]{3,2,1,0:T(8,128)S(1)}, f32[16,4,64,64]{3,2,1,0:T(8,128)}, u32[]{:S(2)}) copy-start(f32[16,4,64,64]{3,2,1,0:T(8,128)} %get-tuple-element.245) | copy-start | bytes 3145732 | tf_op jit(solution)/shard_map/while
  78.3 3.4 %copy-start.2 = (f32[16,4,64,64]{3,2,1,0:T(8,128)}, f32[16,4,64,64]{3,2,1,0:T(8,128)S(1)}, u32[]{:S(2)}) copy-start(f32[16,4,64,64]{3,2,1,0:T(8,128)S(1)} %multiply_add_fusion.8) | copy-start | bytes 3145732 | tf_op jit(solution)/shard_map/while
  81.7 8.2 %copy-start.1 = (f32[16,4,64,64]{3,2,1,0:T(8,128)S(1)}, f32[16,4,64,64]{3,2,1,0:T(8,128)}, u32[]{:S(2)}) copy-start(f32[16,4,64,64]{3,2,1,0:T(8,128)} %get-tuple-element.245) | copy-start | bytes 3145732 | tf_op jit(solution)/shard_map/while
  94.9 8.2 %copy-start.1 = (f32[16,4,64,64]{3,2,1,0:T(8,128)S(1)}, f32[16,4,64,64]{3,2,1,0:T(8,128)}, u32[]{:S(2)}) copy-start(f32[16,4,64,64]{3,2,1,0:T(8,128)} %get-tuple-element.245) | copy-start | bytes 3145732 | tf_op jit(solution)/shard_map/while
  104.7 3.4 %copy-start.2 = (f32[16,4,64,64]{3,2,1,0:T(8,128)}, f32[16,4,64,64]{3,2,1,0:T(8,128)S(1)}, u32[]{:S(2)}) copy-start(f32[16,4,64,64]{3,2,1,0:T(8,128)S(1)} %multiply_add_fusion.8) | copy-start | bytes 3145732 | tf_op jit(solution)/shard_map/while
  108.1 8.2 %copy-start.1 = (f32[16,4,64,64]{3,2,1,0:T(8,128)S(1)}, f32[16,4,64,64]{3,2,1,0:T(8,128)}, u32[]{:S(2)}) copy-start(f32[16,4,64,64]{3,2,1,0:T(8,128)} %get-tuple-element.245) | copy-start | bytes 3145732 | tf_op jit(solution)/shard_map/while
  121.3 8.2 %copy-start.1 = (f32[16,4,64,64]{3,2,1,0:T(8,128)S(1)}, f32[16,4,64,64]{3,2,1,0:T(8,128)}, u32[]{:S(2)}) copy-start(f32[16,4,64,64]{3,2,1,0:T(8,128)} %get-tuple-element.245) | copy-start | bytes 3145732 | tf_op jit(solution)/shard_map/while
  131.0 3.4 %copy-start.2 = (f32[16,4,64,64]{3,2,1,0:T(8,128)}, f32[16,4,64,64]{3,2,1,0:T(8,128)S(1)}, u32[]{:S(2)}) copy-start(f32[16,4,64,64]{3,2,1,0:T(8,128)S(1)} %multiply_add_fusion.8) | copy-start | bytes 3145732 | tf_op jit(solution)/shard_map/while
  147.3 40.1 %all-to-all-start = ((f32[16,128,256]{2,1,0:T(8,128)}), f32[16,128,256]{2,1,0:T(8,128)}, u32[]{:S(2)}, u32[]{:S(2)}) async-start(f32[16,128,256]{2,1,0:T(8,128)} %bitcast.113), calls=%async_computation | async-start | bytes 4194304 | tf_op jit(solution)/shard_map/all_to_all | solution.py:19
  155.5 119.1 %all-gather.3.cloned.1.call-start = ((), (), s32[]{:S(2)}) async-start(), calls=%async_computation.4 | async-start | bytes 9437184 | tf_op jit(solution)/shard_map/all_gather | solution.py:219
  206.7 16.9 %copy-start.5 = (s32[16,8]{0,1:T(8,128)S(1)}, s32[16,8]{0,1:T(8,128)}, u32[]{:S(2)}) copy-start(s32[16,8]{0,1:T(8,128)} %param.30) | copy-start | bytes 1540
  282.9 19.5 %copy-start.6 = (s32[16,8]{0,1:T(8,128)S(1)}, s32[16,8]{0,1:T(8,128)}, u32[]{:S(2)}) copy-start(s32[16,8]{0,1:T(8,128)} %param.31) | copy-start | bytes 1540
  284.1 10.1 %all-to-all-start.2 = ((f32[8,3,1024]{2,1,0:T(4,128)}), f32[8,3,1024]{2,1,0:T(4,128)S(1)}, u32[]{:S(2)}, u32[]{:S(2)}) async-start(f32[8,3,1024]{2,1,0:T(4,128)} %broadcast_in_dim.23), calls=%async_computation.2 | async-start | bytes 262144 | tf_op jit(solution)/shard_map/all_to_all | solution.py:37
  295.4 14.6 %all-to-all-start.3 = ((f32[16,3,128]{2,1,0:T(4,128)}), f32[16,3,128]{2,1,0:T(4,128)S(1)}, u32[]{:S(2)}, u32[]{:S(2)}) async-start(f32[16,3,128]{2,1,0:T(4,128)} %broadcast_in_dim.25), calls=%async_computation.3 | async-start | bytes 65536 | tf_op jit(solution)/shard_map/all_to_all | solution.py:37
  (3 other events, 10.1 us)
Sparse Core Ops, SparseCore 0:
  223.6 50.9 all-gather.2
where the time goes:
time: 321 us; the launch traced here: 319 us
  matrix products  84.9 us (26%)
  waiting for transfers between devices  82.3 us (26%)
  blocking collectives  47.1 us (15%)
  local copies, waits for them, and re-layouts  41.7 us (13%)
  other arithmetic  29.1 us (9%)
  starting transfers between devices  19.2 us (6%)
  between operations  14.4 us (4%)
    dot_general x8, matrix products, step(): jnp.einsum('bhij,bhj->bhi', current, unit_now, precision=lax.Precision.HI...  39.5 us
    all_gather x1, waiting for transfers between devices, shards(): lax.all_gather(normed, 'batch', axis=0, tiled=True)  37.6 us
    all_to_all x1, waiting for transfers between devices, sent_and_summed(): parts = lax.all_to_all(in_blocks(x, dim, size), axis, 0, 0, tiled=True)  31 us
    dot_general x8, matrix products, step(): jnp.einsum('bhij,bhj->bhi', current, recept_now, precision=lax.Precision....  26.8 us
    psum x2, blocking collectives, by_axis(): x = lax.psum(x, axis)  17.2 us
    all_to_all x1, blocking collectives, sent_to_all(): return lax.all_to_all(copies, axis, split_axis=0, concat_axis=0, tiled=True)  16.6 us
    all_to_all x2, waiting for transfers between devices, sent_to_all(): return lax.all_to_all(copies, axis, split_axis=0, concat_axis=0, tiled=True)  13.6 us
    all_gather x1, blocking collectives, shards(): lax.all_gather(proposed_tokens_list, 'batch', axis=0, tiled=True)  13.3 us
  transfers between devices with their start and end apart: 4, of which 4 were waited for; matrix products, arithmetic and copies ran while one was open for 0% of the time, Pallas kernels for 0%

commit v1 on v0

--- a/solution.py
+++ b/solution.py
@@ -4,6 +4,7 @@
 from jax import lax
 from jax.sharding import Mesh
 from jax.sharding import PartitionSpec as P
+from jax.lax import all_gather
 
 HEAD = ("head_0", "head_1")
 HEAD_BATCH = ("head_0", "head_1", "batch")
@@ -22,7 +23,7 @@
 
 def by_axis(x, axes):
     for axis in axes:
-        x = lax.psum(x, axis)
+        x = jnp.sum(all_gather(x, axis_name=axis), axis=0)
     return x
 
 

time: 321 us -> 336 us (1.047)
  blocking collectives: 47.1 us -> 62 us
    all_gather x0 -> x4, blocking collectives: none -> 31.9 us  [by_axis(): x = jnp.sum(all_gather(x, axis_name=axis), axis=0)]
    psum x2 -> x0, blocking collectives: 17.2 us -> none  [by_axis(): x = lax.psum(x, axis)]
where the time goes in v1:
time: 336 us; the launch traced here: 334 us
  matrix products  84.9 us (25%)
  waiting for transfers between devices  82.2 us (24%)
  blocking collectives  62 us (18%)
  local copies, waits for them, and re-layouts  41.6 us (12%)
  other arithmetic  29.1 us (9%)
  starting transfers between devices  19.2 us (6%)
  between operations  14.4 us (4%)
    dot_general x8, matrix products, step(): jnp.einsum('bhij,bhj->bhi', current, unit_now, precision=lax.Precision.HI...  39.5 us
    all_gather x1, waiting for transfers between devices, shards(): lax.all_gather(normed, 'batch', axis=0, tiled=True)  37.5 us
    all_gather x4, blocking collectives, by_axis(): x = jnp.sum(all_gather(x, axis_name=axis), axis=0)  31.9 us
    all_to_all x1, waiting for transfers between devices, sent_and_summed(): parts = lax.all_to_all(in_blocks(x, dim, size), axis, 0, 0, tiled=True)  31 us
    dot_general x8, matrix products, step(): jnp.einsum('bhij,bhj->bhi', current, recept_now, precision=lax.Precision....  26.8 us
    all_to_all x1, blocking collectives, sent_to_all(): return lax.all_to_all(copies, axis, split_axis=0, concat_axis=0, tiled=True)  16.8 us
    all_to_all x2, waiting for transfers between devices, sent_to_all(): return lax.all_to_all(copies, axis, split_axis=0, concat_axis=0, tiled=True)  13.6 us
    all_gather x1, blocking collectives, shards(): lax.all_gather(proposed_tokens_list, 'batch', axis=0, tiled=True)  13.3 us
  transfers between devices with their start and end apart: 4, of which 4 were waited for; matrix products, arithmetic and copies ran while one was open for 0% of the time, Pallas kernels for 0%

profile of v1, /device:TPU:0, one launch (start us, length us, event | category | flops | bytes accessed | tf_op | source)
XLA Modules:
  0.0 333.9 jit_solution(6656109188221150944)
XLA Ops:
  29.0 105.4 %while.12 = (s32[]{:T(128)}, f32[16,4,64,64]{3,2,1,0:T(8,128)}, f32[8,16,4,64]{3,2,1,0:T(4,128)S(1)}, f32[8,16,4,64]{3,2,0,1:T(4,128)}, f32[8,16,4,64]{3,2,1,0:T...) while((s32[]{:T(128)}, f32[16,4,64,64]{3,2,1,0:T(8,128)}, ...), condition=%wide.region_2.3_spmd, body=%wide.region_1.2_spmd.sunk | while | flops 7606274 | bytes 13009081 | solution.py:120
  31.5 4.9 %fusion.54 = f32[16,4,1,64]{3,2,1,0:T(1,128)S(1)} fusion(f32[16,4,64,1]{2,3,1,0:T(1,128)S(1)} %bitcast.122, f32[16,4,64,64]{3,2,1,0:T(8,128)} %get-tuple-element.241), kind=kOutput, calls=%fused_computation.79.clone.1 | convolution fusion | flops 3145728 | bytes 1081344 | tf_op jit(solution)/shard_map/while/body/eval_jaxpr/bhij,bhj->bhi/dot_general | solution.py:111
  44.7 4.9 %fusion.54 = f32[16,4,1,64]{3,2,1,0:T(1,128)S(1)} fusion(f32[16,4,64,1]{2,3,1,0:T(1,128)S(1)} %bitcast.122, f32[16,4,64,64]{3,2,1,0:T(8,128)} %get-tuple-element.241), kind=kOutput, calls=%fused_computation.79.clone.1 | convolution fusion | flops 3145728 | bytes 1081344 | tf_op jit(solution)/shard_map/while/body/eval_jaxpr/bhij,bhj->bhi/dot_general | solution.py:111
  57.9 4.9 %fusion.54 = f32[16,4,1,64]{3,2,1,0:T(1,128)S(1)} fusion(f32[16,4,64,1]{2,3,1,0:T(1,128)S(1)} %bitcast.122, f32[16,4,64,64]{3,2,1,0:T(8,128)} %get-tuple-element.241), kind=kOutput, calls=%fused_computation.79.clone.1 | convolution fusion | flops 3145728 | bytes 1081344 | tf_op jit(solution)/shard_map/while/body/eval_jaxpr/bhij,bhj->bhi/dot_general | solution.py:111
  71.0 4.9 %fusion.54 = f32[16,4,1,64]{3,2,1,0:T(1,128)S(1)} fusion(f32[16,4,64,1]{2,3,1,0:T(1,128)S(1)} %bitcast.122, f32[16,4,64,64]{3,2,1,0:T(8,128)} %get-tuple-element.241), kind=kOutput, calls=%fused_computation.79.clone.1 | convolution fusion | flops 3145728 | bytes 1081344 | tf_op jit(solution)/shard_map/while/body/eval_jaxpr/bhij,bhj->bhi/dot_general | solution.py:111
  84.2 4.9 %fusion.54 = f32[16,4,1,64]{3,2,1,0:T(1,128)S(1)} fusion(f32[16,4,64,1]{2,3,1,0:T(1,128)S(1)} %bitcast.122, f32[16,4,64,64]{3,2,1,0:T(8,128)} %get-tuple-element.241), kind=kOutput, calls=%fused_computation.79.clone.1 | convolution fusion | flops 3145728 | bytes 1081344 | tf_op jit(solution)/shard_map/while/body/eval_jaxpr/bhij,bhj->bhi/dot_general | solution.py:111
  97.4 4.9 %fusion.54 = f32[16,4,1,64]{3,2,1,0:T(1,128)S(1)} fusion(f32[16,4,64,1]{2,3,1,0:T(1,128)S(1)} %bitcast.122, f32[16,4,64,64]{3,2,1,0:T(8,128)} %get-tuple-element.241), kind=kOutput, calls=%fused_computation.79.clone.1 | convolution fusion | flops 3145728 | bytes 1081344 | tf_op jit(solution)/shard_map/while/body/eval_jaxpr/bhij,bhj->bhi/dot_general | solution.py:111
  110.6 4.9 %fusion.54 = f32[16,4,1,64]{3,2,1,0:T(1,128)S(1)} fusion(f32[16,4,64,1]{2,3,1,0:T(1,128)S(1)} %bitcast.122, f32[16,4,64,64]{3,2,1,0:T(8,128)} %get-tuple-element.241), kind=kOutput, calls=%fused_computation.79.clone.1 | convolution fusion | flops 3145728 | bytes 1081344 | tf_op jit(solution)/shard_map/while/body/eval_jaxpr/bhij,bhj->bhi/dot_general | solution.py:111
  123.8 4.9 %fusion.54 = f32[16,4,1,64]{3,2,1,0:T(1,128)S(1)} fusion(f32[16,4,64,1]{2,3,1,0:T(1,128)S(1)} %bitcast.122, f32[16,4,64,64]{3,2,1,0:T(8,128)} %get-tuple-element.241), kind=kOutput, calls=%fused_computation.79.clone.1 | convolution fusion | flops 3145728 | bytes 1081344 | tf_op jit(solution)/shard_map/while/body/eval_jaxpr/bhij,bhj->bhi/dot_general | solution.py:111
  139.9 4.2 %fusion.5 = f32[128,4096]{1,0:T(8,128)} fusion(bf16[256,4096]{1,0:T(8,128)(2,1)S(1)} %copy-done, f32[128,256]{1,0:T(8,128)S(1)} %reshape.139, bf16[128,4096]{1,0:T(8,128)(2,1)S(1)} %copy-done.3, bf16[4096,256]{1,0:T(8,128)(2,1)} %param.21), kind=kOutput, calls=%fused_computation.18 | convolution fusion | flops 537034752 | bytes 7471104 | tf_op jit(solution)/shard_map/dot_general | solution.py:201
  147.3 8.2 %all-to-all-start = ((f32[16,128,256]{2,1,0:T(8,128)}), f32[16,128,256]{2,1,0:T(8,128)}, u32[]{:S(2)}, u32[]{:S(2)}) async-start(f32[16,128,256]{2,1,0:T(8,128)} %bitcast.117), calls=%async_computation | async-start | bytes 4194304 | tf_op jit(solution)/shard_map/all_to_all | solution.py:20
  156.3 31.0 %all-to-all-done = f32[16,128,256]{2,1,0:T(8,128)} async-done(((f32[16,128,256]{2,1,0:T(8,128)}), f32[16,128,256]{2,1,0:T(8,128)}, u32[]{:S(2)}, u32[]{:S(2)}) %all-to-all-start) | async-done | bytes 2097184 | tf_op jit(solution)/shard_map/all_to_all | solution.py:20
  189.2 8.7 %all-gather.4 = f32[4,1,128]{2,1,0:T(1,128)S(1)} all-gather(f32[1,1,128]{2,1,0:T(1,128)S(1)} %bitcast.142), channel_id=2, replica_groups=mesh['head_0'=4,'head_1'=4,'batch'=8] {'head_0'}, dimensions={0}, use_global_device_ids=true | all-gather | bytes 2560 | tf_op jit(solution)/shard_map/all_gather | solution.py:26
  197.9 7.0 %all-gather.5 = f32[4,1,128]{2,1,0:T(1,128)S(1)} all-gather(f32[1,1,128]{2,1,0:T(1,128)S(1)} %bitcast.143), channel_id=3, replica_groups=mesh['head_0'=4,'head_1'=4,'batch'=8] {'head_1'}, dimensions={0}, use_global_device_ids=true | all-gather | bytes 2560 | tf_op jit(solution)/shard_map/all_gather | solution.py:26
  204.9 7.3 %all-gather.6 = f32[4,1,128]{2,1,0:T(1,128)S(1)} all-gather(f32[1,1,128]{2,1,0:T(1,128)S(1)} %bitcast.141), channel_id=4, replica_groups=mesh['head_0'=4,'head_1'=4,'batch'=8] {'head_0'}, dimensions={0}, use_global_device_ids=true | all-gather | bytes 2560 | tf_op jit(solution)/shard_map/all_gather | solution.py:26
  212.2 9.0 %all-gather.7 = f32[4,1,128]{2,1,0:T(1,128)S(1)} all-gather(f32[1,1,128]{2,1,0:T(1,128)S(1)} %bitcast.144), channel_id=5, replica_groups=mesh['head_0'=4,'head_1'=4,'batch'=8] {'head_1'}, dimensions={0}, use_global_device_ids=true | all-gather | bytes 2560 | tf_op jit(solution)/shard_map/all_gather | solution.py:26
  221.7 16.8 %all_to_all.20 = bf16[16,128,256]{1,2,0:T(8,128)(2,1)} all-to-all(bf16[16,128,256]{1,2,0:T(8,128)(2,1)S(1)} %broadcast_in_dim.21), channel_id=1, replica_groups=mesh['head_0'=4,'head_1'=4,'batch'=8] {'head_0','head_1'}, dimensions={0} | all-to-all | bytes 2097152 | tf_op jit(solution)/shard_map/all_to_all | solution.py:38
  238.6 13.3 %all-gather.8 = s32[8,16,8]{1,2,0:T(8,128)S(1)} all-gather(s32[1,16,8]{1,2,0:T(8,128)S(1)} %bitcast.140), channel_id=1, replica_groups=mesh['head_0'=4,'head_1'=4,'batch'=8] {'batch'}, dimensions={0}, use_global_device_ids=true | all-gather | bytes 4608 | tf_op jit(solution)/shard_map/all_gather | solution.py:221
  252.0 37.5 %all-gather.11.cloned.1.call-done = bf16[1024,4096]{0,1:T(8,128)(2,1)} async-done(((bf16[128,4096]{0,1:T(8,128)(2,1)}), bf16[1024,4096]{0,1:T(8,128)(2,1)}) %all-gather.11.cloned.1.call-update) | async-done | bytes 8388624 | tf_op jit(solution)/shard_map/all_gather | solution.py:220
  289.5 8.3 %fusion.23 = (f32[1024]{0:T(1024)S(1)}, f32[1024,512]{0,1:T(8,128)S(1)}) fusion(bf16[1024,4096]{0,1:T(8,128)(2,1)} %all-gather.11.cloned.1.call-done, bf16[4096,512]{1,0:T(8,128)(2,1)} %param.29), kind=kOutput, calls=%fused_computation.78 | convolution fusion | flops 4295490560 | bytes 14684160 | tf_op jit(solution)/shard_map/dot_general | solution.py:223
  299.1 4.0 %all-to-all-start.2 = ((f32[8,3,1024]{2,1,0:T(4,128)}), f32[8,3,1024]{2,1,0:T(4,128)S(1)}, u32[]{:S(2)}, u32[]{:S(2)}) async-start(f32[8,3,1024]{2,1,0:T(4,128)} %broadcast_in_dim.23), calls=%async_computation.2 | async-start | bytes 262144 | tf_op jit(solution)/shard_map/all_to_all | solution.py:38
  303.0 6.1 %all-to-all-done.2 = f32[8,3,1024]{2,1,0:T(4,128)S(1)} async-done(((f32[8,3,1024]{2,1,0:T(4,128)}), f32[8,3,1024]{2,1,0:T(4,128)S(1)}, u32[]{:S(2)}, u32[]{:S(2)}) %all-to-all-start.2) | async-done | bytes 98336 | tf_op jit(solution)/shard_map/all_to_all | solution.py:38
  310.4 7.0 %all-to-all-start.3 = ((f32[16,3,128]{2,1,0:T(4,128)}), f32[16,3,128]{2,1,0:T(4,128)S(1)}, u32[]{:S(2)}, u32[]{:S(2)}) async-start(f32[16,3,128]{2,1,0:T(4,128)} %broadcast_in_dim.25), calls=%async_computation.3 | async-start | bytes 65536 | tf_op jit(solution)/shard_map/all_to_all | solution.py:38
  317.4 7.5 %all-to-all-done.3 = f32[16,3,128]{2,1,0:T(4,128)S(1)} async-done(((f32[16,3,128]{2,1,0:T(4,128)}), f32[16,3,128]{2,1,0:T(4,128)S(1)}, u32[]{:S(2)}, u32[]{:S(2)}) %all-to-all-start.3) | async-done | bytes 24608 | tf_op jit(solution)/shard_map/all_to_all | solution.py:38
  (212 shorter events, 103.7 us)
Async XLA Ops:
  7.2 132.7 %copy-start = (bf16[256,4096]{1,0:T(8,128)(2,1)S(1)}, bf16[256,4096]{1,0:T(8,128)(2,1)}, u32[]{:S(2)}) copy-start(bf16[256,4096]{1,0:T(8,128)(2,1)} %param.27) | copy-start | bytes 6291460
  7.2 5.1 %copy-start.3 = (bf16[128,4096]{1,0:T(8,128)(2,1)S(1)}, bf16[128,4096]{1,0:T(8,128)(2,1)}, u32[]{:S(2)}) copy-start(bf16[128,4096]{1,0:T(8,128)(2,1)} %param.17) | copy-start | bytes 3145732
  14.3 3.8 %copy-start.7 = (f32[256]{0:T(256)S(1)}, f32[256]{0:T(256)}, u32[]{:S(2)}) copy-start(f32[256]{0:T(256)} %param.24) | copy-start | bytes 3076
  29.0 105.5 %copy-start.4 = (f32[16,8,4]{2,1,0:T(8,128)S(1)}, f32[16,8,4]{2,1,0:T(8,128)}, u32[]{:S(2)}) copy-start(f32[16,8,4]{2,1,0:T(8,128)} %get-tuple-element.108) | copy-start | bytes 6148
  29.0 106.1 %copy-start.8 = (f32[256]{0:T(256)S(1)}, f32[256]{0:T(256)}, u32[]{:S(2)}) copy-start(f32[256]{0:T(256)} %param.25) | copy-start | bytes 3076
  29.0 8.2 %copy-start.1 = (f32[16,4,64,64]{3,2,1,0:T(8,128)S(1)}, f32[16,4,64,64]{3,2,1,0:T(8,128)}, u32[]{:S(2)}) copy-start(f32[16,4,64,64]{3,2,1,0:T(8,128)} %get-tuple-element.241) | copy-start | bytes 3145732 | tf_op jit(solution)/shard_map/while
  38.7 3.4 %copy-start.2 = (f32[16,4,64,64]{3,2,1,0:T(8,128)}, f32[16,4,64,64]{3,2,1,0:T(8,128)S(1)}, u32[]{:S(2)}) copy-start(f32[16,4,64,64]{3,2,1,0:T(8,128)S(1)} %multiply_add_fusion.8) | copy-start | bytes 3145732 | tf_op jit(solution)/shard_map/while
  42.1 8.2 %copy-start.1 = (f32[16,4,64,64]{3,2,1,0:T(8,128)S(1)}, f32[16,4,64,64]{3,2,1,0:T(8,128)}, u32[]{:S(2)}) copy-start(f32[16,4,64,64]{3,2,1,0:T(8,128)} %get-tuple-element.241) | copy-start | bytes 3145732 | tf_op jit(solution)/shard_map/while
  55.3 8.2 %copy-start.1 = (f32[16,4,64,64]{3,2,1,0:T(8,128)S(1)}, f32[16,4,64,64]{3,2,1,0:T(8,128)}, u32[]{:S(2)}) copy-start(f32[16,4,64,64]{3,2,1,0:T(8,128)} %get-tuple-element.241) | copy-start | bytes 3145732 | tf_op jit(solution)/shard_map/while
  65.1 3.4 %copy-start.2 = (f32[16,4,64,64]{3,2,1,0:T(8,128)}, f32[16,4,64,64]{3,2,1,0:T(8,128)S(1)}, u32[]{:S(2)}) copy-start(f32[16,4,64,64]{3,2,1,0:T(8,128)S(1)} %multiply_add_fusion.8) | copy-start | bytes 3145732 | tf_op jit(solution)/shard_map/while
  68.5 8.2 %copy-start.1 = (f32[16,4,64,64]{3,2,1,0:T(8,128)S(1)}, f32[16,4,64,64]{3,2,1,0:T(8,128)}, u32[]{:S(2)}) copy-start(f32[16,4,64,64]{3,2,1,0:T(8,128)} %get-tuple-element.241) | copy-start | bytes 3145732 | tf_op jit(solution)/shard_map/while
  81.7 8.2 %copy-start.1 = (f32[16,4,64,64]{3,2,1,0:T(8,128)S(1)}, f32[16,4,64,64]{3,2,1,0:T(8,128)}, u32[]{:S(2)}) copy-start(f32[16,4,64,64]{3,2,1,0:T(8,128)} %get-tuple-element.241) | copy-start | bytes 3145732 | tf_op jit(solution)/shard_map/while
  91.5 3.4 %copy-start.2 = (f32[16,4,64,64]{3,2,1,0:T(8,128)}, f32[16,4,64,64]{3,2,1,0:T(8,128)S(1)}, u32[]{:S(2)}) copy-start(f32[16,4,64,64]{3,2,1,0:T(8,128)S(1)} %multiply_add_fusion.8) | copy-start | bytes 3145732 | tf_op jit(solution)/shard_map/while
  94.9 8.2 %copy-start.1 = (f32[16,4,64,64]{3,2,1,0:T(8,128)S(1)}, f32[16,4,64,64]{3,2,1,0:T(8,128)}, u32[]{:S(2)}) copy-start(f32[16,4,64,64]{3,2,1,0:T(8,128)} %get-tuple-element.241) | copy-start | bytes 3145732 | tf_op jit(solution)/shard_map/while
  104.7 3.4 %copy-start.2 = (f32[16,4,64,64]{3,2,1,0:T(8,128)}, f32[16,4,64,64]{3,2,1,0:T(8,128)S(1)}, u32[]{:S(2)}) copy-start(f32[16,4,64,64]{3,2,1,0:T(8,128)S(1)} %multiply_add_fusion.8) | copy-start | bytes 3145732 | tf_op jit(solution)/shard_map/while
  108.1 8.2 %copy-start.1 = (f32[16,4,64,64]{3,2,1,0:T(8,128)S(1)}, f32[16,4,64,64]{3,2,1,0:T(8,128)}, u32[]{:S(2)}) copy-start(f32[16,4,64,64]{3,2,1,0:T(8,128)} %get-tuple-element.241) | copy-start | bytes 3145732 | tf_op jit(solution)/shard_map/while
  121.2 8.2 %copy-start.1 = (f32[16,4,64,64]{3,2,1,0:T(8,128)S(1)}, f32[16,4,64,64]{3,2,1,0:T(8,128)}, u32[]{:S(2)}) copy-start(f32[16,4,64,64]{3,2,1,0:T(8,128)} %get-tuple-element.241) | copy-start | bytes 3145732 | tf_op jit(solution)/shard_map/while
  131.0 3.4 %copy-start.2 = (f32[16,4,64,64]{3,2,1,0:T(8,128)}, f32[16,4,64,64]{3,2,1,0:T(8,128)S(1)}, u32[]{:S(2)}) copy-start(f32[16,4,64,64]{3,2,1,0:T(8,128)S(1)} %multiply_add_fusion.8) | copy-start | bytes 3145732 | tf_op jit(solution)/shard_map/while
  147.3 40.1 %all-to-all-start = ((f32[16,128,256]{2,1,0:T(8,128)}), f32[16,128,256]{2,1,0:T(8,128)}, u32[]{:S(2)}, u32[]{:S(2)}) async-start(f32[16,128,256]{2,1,0:T(8,128)} %bitcast.117), calls=%async_computation | async-start | bytes 4194304 | tf_op jit(solution)/shard_map/all_to_all | solution.py:20
  155.5 134.0 %all-gather.11.cloned.1.call-start = ((), (), s32[]{:S(2)}) async-start(), calls=%async_computation.4 | async-start | bytes 9437184 | tf_op jit(solution)/shard_map/all_gather | solution.py:220
  221.5 17.1 %copy-start.5 = (s32[16,8]{0,1:T(8,128)S(1)}, s32[16,8]{0,1:T(8,128)}, u32[]{:S(2)}) copy-start(s32[16,8]{0,1:T(8,128)} %param.30) | copy-start | bytes 1540
  297.8 19.5 %copy-start.6 = (s32[16,8]{0,1:T(8,128)S(1)}, s32[16,8]{0,1:T(8,128)}, u32[]{:S(2)}) copy-start(s32[16,8]{0,1:T(8,128)} %param.31) | copy-start | bytes 1540
  299.1 10.1 %all-to-all-start.2 = ((f32[8,3,1024]{2,1,0:T(4,128)}), f32[8,3,1024]{2,1,0:T(4,128)S(1)}, u32[]{:S(2)}, u32[]{:S(2)}) async-start(f32[8,3,1024]{2,1,0:T(4,128)} %broadcast_in_dim.23), calls=%async_computation.2 | async-start | bytes 262144 | tf_op jit(solution)/shard_map/all_to_all | solution.py:38
  310.4 14.6 %all-to-all-start.3 = ((f32[16,3,128]{2,1,0:T(4,128)}), f32[16,3,128]{2,1,0:T(4,128)S(1)}, u32[]{:S(2)}, u32[]{:S(2)}) async-start(f32[16,3,128]{2,1,0:T(4,128)} %broadcast_in_dim.25), calls=%async_computation.3 | async-start | bytes 65536 | tf_op jit(solution)/shard_map/all_to_all | solution.py:38
  (3 other events, 10.1 us)
Sparse Core Ops, SparseCore 0:
  238.7 50.8 all-gather.10
